TPU v7x, 32 devices: a whole 2x2x4 slice. The times are simulated.
32 devices in a mesh: batch: 4 (over z), rows: 8 (over y, x, core).
Axes of the slice: x: 2, y: 2, z: 4, core: 2. Of those that a mesh axis runs over, the one named last changes fastest.
Arguments:
- level_two: bfloat16 [8, 64, 256, 256], P('batch', 'rows'), parts along dimension 0, may hold values from -130 to 130
- level_three: bfloat16 [8, 32, 128, 512], P('batch', 'rows'), parts along dimension 0, may hold values from -130 to 130
- level_four: bfloat16 [8, 16, 64, 1024], P('batch', 'rows'), parts along dimension 0, may hold values from -130 to 130
- level_five: bfloat16 [8, 8, 32, 2048], P('batch', 'rows'), parts along dimension 0, may hold values from -130 to 130
- lateral_two: bfloat16 [256, 256], replicated, may hold values from -0.375 to 0.375
- lateral_three: bfloat16 [512, 256], replicated, may hold values from -0.25 to 0.25
- lateral_four: bfloat16 [1024, 256], replicated, may hold values from -0.1875 to 0.1875
- lateral_five: bfloat16 [2048, 256], replicated, may hold values from -0.125 to 0.125
- lateral_bias: float32 [4, 256], replicated, may hold values from -4 to 4
- smooth_weight: bfloat16 [4, 3, 768, 256], replicated, may hold values from -0.125 to 0.125
- norm_gain: float32 [4, 256], replicated, may hold values from 0.5 to 1.5
- norm_shift: float32 [4, 256], replicated, may hold values from -2 to 2
Outputs:
- pyramid_two: bfloat16 [8, 64, 256, 256], P('batch', 'rows'), parts along dimension 0
- pyramid_three: bfloat16 [8, 32, 128, 256], P('batch', 'rows'), parts along dimension 0
- pyramid_four: bfloat16 [8, 16, 64, 256], P('batch', 'rows'), parts along dimension 0
- pyramid_five: bfloat16 [8, 8, 32, 256], P('batch', 'rows'), parts along dimension 0
There are 4 independent parts, one for each index of `batch`. A program takes and returns all parts, laid end to end along the dimension named above; an argument that names none is the same for every part. Nothing has to cross between parts.
All inputs are finite; a program needn't handle non-finite values.
Results may differ from a plain program's by a relative error of at most 0.0054.
Values may be sent and summed in bfloat16 or wider, within the bound.
No kernel may reach another device: no remote copies, remote signals or barrier semaphores. Data moves between devices by JAX's collectives and lax.ppermute only.
A program may use at most 128 MiB of HBM per device.

v0:
```python
import functools

import jax
import jax.numpy as jnp
from jax import lax
from jax.experimental import pallas as pl
from jax.experimental.pallas import tpu as pltpu
from jax.sharding import PartitionSpec as P


GROUPS = 32
EPSILON = 1e-05
F32 = jnp.float32
BF16 = jnp.bfloat16
MIB = 1 << 20


def dot(a, b):
    return jnp.dot(a, b, preferred_element_type=F32)


def flat(v):
    return v.reshape(-1, v.shape[-1])


def segments(widths):
    offsets, total = [], 0
    for width in widths:
        offsets.append(total)
        total += width
    return offsets, total


def lateral_kernel(
    x2, x3, x4, x5, w2, w3, w4, w5, bias,
    lat3, lat4, lat5, downward, upward, downward2, upward2,
    edge2, v3, v4, v5, m2, m3, m4, m5, offset, sems,
):
    rows2 = x2.shape[1]
    moves = [
        (x5, v5), (w5, m5), (x4, v4), (w4, m4), (x3, v3), (w3, m3),
        (x2.at[:, 0], edge2.at[0]), (x2.at[:, rows2 - 1], edge2.at[1]), (w2, m2),
        (bias, offset),
    ]
    copies = [
        pltpu.make_async_copy(src, dst, sems.at[n]) for n, (src, dst) in enumerate(moves)
    ]
    for c in copies:
        c.start()
    widths = (x3.shape[2], x4.shape[2], x5.shape[2])
    offsets, _ = segments(widths)
    copies[9].wait()
    first = 0
    for level, v, m, out in ((3, v5, m5, lat5), (2, v4, m4, lat4), (1, v3, m3, lat3)):
        copies[first].wait()
        copies[first + 1].wait()
        first += 2
        res = dot(flat(v[...]), m[...]) + offset[level : level + 1, :]
        res = res.reshape(out.shape)
        out[...] = res
        seg = slice(offsets[level - 1], offsets[level - 1] + widths[level - 1])
        downward[:, seg, :] = res[:, out.shape[1] - 1].astype(BF16)
        upward[:, seg, :] = res[:, 0].astype(BF16)
    for n in (6, 7, 8):
        copies[n].wait()
    for side, ref in ((0, upward2), (1, downward2)):
        res = dot(flat(edge2[side]), m2[...]) + offset[0:1, :]
        ref[...] = res.reshape(ref.shape).astype(BF16)


def fill_weights(table):
    _, fine, twice = table.shape
    coarse = twice // 2
    row = lax.broadcasted_iota(jnp.int32, (fine, twice), 0)
    col = lax.broadcasted_iota(jnp.int32, (fine, twice), 1)
    second = col >= coarse
    col = jnp.where(second, col - coarse, col)
    near = row // 2
    far = jnp.clip(jnp.where(row % 2 == 0, near - 1, near + 1), 0, coarse - 1)
    base = jnp.where(col == near, 0.75, 0.0) + jnp.where(col == far, 0.25, 0.0)
    for n, (a, b) in enumerate(((0.25, 0.75), (0.75, 0.25), (0.0, 1.0), (1.0, 0.0))):
        table[n] = (base * jnp.where(second, b, a)).astype(BF16)


def put(cat, image, slot, acc):
    cols, channels = acc.shape
    row = lax.broadcasted_iota(jnp.int32, (8, channels), 0)
    left = pltpu.roll(acc, 1, 0)
    left = jnp.concatenate([jnp.where(row == 0, 0.0, left[:8]), left[8:]], 0)
    right = pltpu.roll(acc, cols - 1, 0)
    right = jnp.concatenate([right[:-8], jnp.where(row == 7, 0.0, right[-8:])], 0)
    cat[image, slot, :, 0:channels] = left.astype(BF16)
    cat[image, slot, :, channels : 2 * channels] = acc.astype(BF16)
    cat[image, slot, :, 2 * channels : 3 * channels] = right.astype(BF16)


def note_sums(stats, at, res):
    part = res.reshape(-1, 8, res.shape[-1])
    stats[at : at + 1, :] = jnp.sum(jnp.sum(part, axis=0), axis=0, keepdims=True)
    stats[at + 1 : at + 2, :] = jnp.sum(jnp.sum(part * part, axis=0), axis=0, keepdims=True)


def coarse_kernel(
    ends, x2, w2, bias, lat3, lat4, lat5, above, below, smooth,
    conv3, conv4, conv5, stats, cat2, rim2, sw2,
    v2, m2, sw, cat3, cat4, cat5, u2, u3, u4, sems,
):
    copies = [pltpu.make_async_copy(w2, m2, sems.at[0])]
    images, rows2, _, _ = x2.shape
    for i in range(images):
        copies.append(pltpu.make_async_copy(x2.at[i], v2.at[i], sems.at[1 + i]))
    for level in (1, 2, 3, 0):
        copies.append(
            pltpu.make_async_copy(
                smooth.at[level],
                sw.at[level - 1] if level else sw2,
                sems.at[1 + images + level],
            )
        )
    for c in copies:
        c.start()
    is_first = ends[0] == 1
    is_last = ends[1] == 1
    cats = (cat2, cat3, cat4, cat5)
    tables = (u2, u3, u4)
    lats = (None, lat3, lat4, lat5)
    channels = lat3.shape[-1]
    for table in tables:
        fill_weights(table)
    offsets, _ = segments(tuple(cat.shape[2] for cat in cats[1:]))

    def raised(level, image, start, which):
        pair = cats[level + 1][image, pl.ds(start, 2), :, channels : 2 * channels]
        return dot(tables[level][which], flat(pair))

    for level in (3, 2, 1):
        height, cols = lats[level].shape[1:3]
        seg = slice(offsets[level - 1], offsets[level - 1] + cols)
        for image in range(images):
            for slot, source, gone, which in (
                (0, above, is_first, 1),
                (height + 1, below, is_last, 0),
            ):
                acc = source[image, seg, :].astype(F32)
                if level < 3:
                    acc = acc + raised(level, image, slot // 2, which)
                put(cats[level], image, slot, jnp.where(gone, 0.0, acc))
            for f in range(height):
                acc = lats[level][image, f]
                if level < 3:
                    which = f % 2
                    if f == 0:
                        which = jnp.where(is_first, 2, which)
                    if f == height - 1:
                        which = jnp.where(is_last, 3, which)
                    acc = acc + raised(level, image, (f + 1) // 2, which)
                put(cats[level], image, f + 1, acc)
    copies[0].wait()
    for image in range(images):
        rim2[0, image] = raised(0, image, 0, 1)
        rim2[1, image] = raised(0, image, rows2 // 2, 0)
        copies[1 + image].wait()

        def pair_rows(j, carry, image=image):
            for odd in range(2):
                f = 2 * j + odd
                if odd:
                    which = jnp.where(jnp.logical_and(is_last, f == rows2 - 1), 3, 1)
                else:
                    which = jnp.where(jnp.logical_and(is_first, f == 0), 2, 0)
                acc = dot(v2[image, f], m2[...]) + bias[0:1, :]
                acc = acc + raised(0, image, j + odd, which)
                put(cat2, image, f, acc)
            return carry

        lax.fori_loop(0, rows2 // 2, pair_rows, 0)

    for level, out in ((1, conv3), (2, conv4), (3, conv5)):
        copies[images + level].wait()
        height = out.shape[1]
        lhs = lambda a: flat(cats[level][:, a : a + height])
        acc = dot(lhs(0), sw[level - 1, 0])
        acc = acc + dot(lhs(1), sw[level - 1, 1])
        acc = acc + dot(lhs(2), sw[level - 1, 2])
        acc = acc.reshape(images, -1, channels)
        out[...] = acc.reshape(out.shape)
        for image in range(images):
            note_sums(stats, 2 * (images * (level - 1) + image), acc[image])
    copies[images + 4].wait()


def fine_kernel(ends, cat2, rim2, sw2, above2, below2, coarse_stats, conv2, stats, halo):
    images, rows2, cols2, _ = cat2.shape
    channels = conv2.shape[-1]
    step = 4 if rows2 % 4 == 0 else 2
    stats[2 * images :, :] = coarse_stats[...]
    for image in range(images):
        for side, source in ((0, above2), (1, below2)):
            acc = source[image].astype(F32) + rim2[side, image]
            put(halo, side, image, jnp.where(ends[side] == 1, 0.0, acc))
    for image in range(images):
        total = square = jnp.zeros((8, channels), F32)
        for r in range(0, rows2, step):
            acc = None
            for tap in range(3):
                low, high = r + tap - 1, r + tap - 1 + step
                lhs = cat2[image, max(low, 0) : min(high, rows2)]
                if low < 0:
                    lhs = jnp.concatenate([halo[0, image][None], lhs], 0)
                if high > rows2:
                    lhs = jnp.concatenate([lhs, halo[1, image][None]], 0)
                res = dot(flat(lhs), sw2[tap])
                acc = res if acc is None else acc + res
            conv2[image, r : r + step] = acc.reshape(step, cols2, channels)
            part = acc.reshape(-1, 8, channels)
            total = total + jnp.sum(part, axis=0)
            square = square + jnp.sum(part * part, axis=0)
        stats[2 * image : 2 * image + 1, :] = jnp.sum(total, axis=0, keepdims=True)
        stats[2 * image + 1 : 2 * image + 2, :] = jnp.sum(square, axis=0, keepdims=True)


def norm_kernel(
    conv2, conv3, conv4, conv5, totals, gain, shift,
    out2, out3, out4, out5,
    s2, s3, s4, s5, sems, *, strips,
):
    channels = conv2.shape[-1]
    width = channels // GROUPS
    row = lax.broadcasted_iota(jnp.int32, (channels, channels), 0) // width
    col = lax.broadcasted_iota(jnp.int32, (channels, channels), 1) // width
    same = jnp.where(row == col, 1.0, 0.0).astype(F32)
    grouped = jnp.dot(
        totals[...], same, precision=lax.Precision.HIGHEST, preferred_element_type=F32
    )
    images = conv2.shape[0]
    copies = []
    levels = ((conv2, s2, out2), (conv3, s3, out3), (conv4, s4, out4), (conv5, s5, out5))
    for level, (conv, stage, out) in enumerate(levels):
        entries = float(conv.shape[1] * strips * conv.shape[2] * width)
        for image in range(images):
            at = 2 * (images * level + image)
            mean = grouped[at : at + 1, :] / entries
            variance = grouped[at + 1 : at + 2, :] / entries - mean * mean
            scale = lax.rsqrt(variance + EPSILON) * gain[level : level + 1, :]
            offset = shift[level : level + 1, :]
            height = conv.shape[1]
            block = min(height, 4)
            for r in range(0, height, block):
                part = flat(conv[image, r : r + block])
                done = ((part - mean) * scale + offset).astype(BF16)
                stage[image, r : r + block] = done.reshape(block, conv.shape[2], channels)
                copy = pltpu.make_async_copy(
                    stage.at[image, pl.ds(r, block)],
                    out.at[image, pl.ds(r, block)],
                    sems.at[len(copies)],
                )
                copy.start()
                copies.append(copy)
    for copy in copies:
        copy.wait()


def total_over(x, axis):
    count = lax.axis_size(axis)
    if count & (count - 1):
        return lax.psum(x, axis)
    step = 1
    while step < count:
        x = x + lax.ppermute(x, axis, [(i, i ^ step) for i in range(count)])
        step *= 2
    return x


def per_device(
    level_two, level_three, level_four, level_five,
    lateral_two, lateral_three, lateral_four, lateral_five,
    lateral_bias, smooth_weight, norm_gain, norm_shift,
):
    position = lax.axis_index("rows")
    strips = lax.axis_size("rows")
    levels = (level_two, level_three, level_four, level_five)
    laterals = (lateral_two, lateral_three, lateral_four, lateral_five)
    levels = tuple(pltpu.with_memory_space_constraint(v, pltpu.HBM) for v in levels)
    laterals = tuple(pltpu.with_memory_space_constraint(v, pltpu.HBM) for v in laterals)
    smooth = pltpu.with_memory_space_constraint(smooth_weight, pltpu.HBM)
    images = level_two.shape[0]
    channels = lateral_two.shape[1]
    widths = tuple(v.shape[2] for v in levels)
    heights = tuple(v.shape[1] for v in levels)
    _, pack = segments(widths[1:])
    hbm = pl.BlockSpec(memory_space=pltpu.HBM)
    vmem = pl.BlockSpec(memory_space=pltpu.VMEM)
    smem = pl.BlockSpec(memory_space=pltpu.SMEM)
    like = lambda v: pltpu.VMEM(v.shape, v.dtype)
    shape = jax.ShapeDtypeStruct
    maps = [shape((images, heights[k], widths[k], channels), F32) for k in range(4)]
    packed = shape((images, pack, channels), BF16)
    packed2 = shape((images, widths[0], channels), BF16)
    lat3, lat4, lat5, downward, upward, downward2, upward2 = pl.pallas_call(
        lateral_kernel,
        out_shape=(maps[1], maps[2], maps[3], packed, packed, packed2, packed2),
        in_specs=[hbm] * 9,
        out_specs=[vmem] * 7,
        scratch_shapes=[
            pltpu.VMEM((2, images) + level_two.shape[2:], level_two.dtype),
            like(level_three), like(level_four), like(level_five),
            like(lateral_two), like(lateral_three), like(lateral_four), like(lateral_five),
            like(lateral_bias), pltpu.SemaphoreType.DMA((10,)),
        ],
        compiler_params=pltpu.CompilerParams(vmem_limit_bytes=20 * MIB),
        name="laterals",
    )(*levels, *laterals, pltpu.with_memory_space_constraint(lateral_bias, pltpu.HBM))
    ends = strips - 1
    from_above = lambda v: lax.ppermute(v, "rows", [(i, i + 1) for i in range(ends)])
    from_below = lambda v: lax.ppermute(v, "rows", [(i + 1, i) for i in range(ends)])
    above, below = from_above(downward), from_below(upward)
    above2, below2 = from_above(downward2), from_below(upward2)
    flags = jnp.stack([position == 0, position == ends]).astype(jnp.int32)
    cat = lambda k: pltpu.VMEM((images, heights[k] + 2, widths[k], 3 * channels), BF16)
    table = lambda k: pltpu.VMEM((4, widths[k], 2 * widths[k + 1]), BF16)
    conv3, conv4, conv5, coarse_stats, cat2, rim2, sw2 = pl.pallas_call(
        coarse_kernel,
        out_shape=(
            maps[1], maps[2], maps[3], shape((6 * images, channels), F32),
            shape((images, heights[0], widths[0], 3 * channels), BF16),
            shape((2, images, widths[0], channels), F32),
            shape(smooth_weight.shape[1:], BF16),
        ),
        in_specs=[smem, hbm, hbm] + [vmem] * 6 + [hbm],
        out_specs=[vmem] * 7,
        scratch_shapes=[
            like(level_two), like(lateral_two),
            pltpu.VMEM((3,) + smooth_weight.shape[1:], BF16),
            cat(1), cat(2), cat(3), table(0), table(1), table(2),
            pltpu.SemaphoreType.DMA((5 + images,)),
        ],
        compiler_params=pltpu.CompilerParams(vmem_limit_bytes=24 * MIB),
        name="merge_coarse",
    )(flags, levels[0], laterals[0], lateral_bias, lat3, lat4, lat5, above, below, smooth)
    conv2, stats = pl.pallas_call(
        fine_kernel,
        out_shape=(maps[0], shape((8 * images, channels), F32)),
        in_specs=[smem] + [vmem] * 6,
        out_specs=[vmem] * 2,
        scratch_shapes=[pltpu.VMEM((2, images, widths[0], 3 * channels), BF16)],
        compiler_params=pltpu.CompilerParams(vmem_limit_bytes=24 * MIB),
        name="conv_fine",
    )(flags, cat2, rim2, sw2, above2, below2, coarse_stats)
    convs = (conv2, conv3, conv4, conv5)
    totals = total_over(stats, "rows")
    outs = [jax.ShapeDtypeStruct(m.shape, BF16) for m in maps]
    count = images * sum(h // min(h, 4) for h in heights)
    return tuple(
        pl.pallas_call(
            functools.partial(norm_kernel, strips=strips),
            out_shape=tuple(outs),
            in_specs=[vmem] * 7,
            out_specs=[hbm] * 4,
            scratch_shapes=[like(o) for o in outs] + [pltpu.SemaphoreType.DMA((count,))],
            compiler_params=pltpu.CompilerParams(vmem_limit_bytes=20 * MIB),
            name="normalize",
        )(*convs, totals, norm_gain, norm_shift)
    )


def solution(mesh):
    split = P("batch", "rows", None, None)
    return jax.shard_map(
        per_device,
        mesh=mesh,
        in_specs=(split,) * 4 + (P(),) * 8,
        out_specs=(split,) * 4,
        check_vma=False,
    )
```

profile of v0, /device:TPU:0, one launch (start us, length us, event | category | flops | bytes accessed | tf_op | source)
XLA Modules:
  0.0 49.1 jit_solution(18368464205688998054)
XLA Ops:
  0.6 0.0 copy-start
  0.6 3.9 %laterals.1 = (f32[2,4,128,256]{3,2,1,0:T(8,128)S(1)}, f32[2,2,64,256]{3,2,1,0:T(8,128)S(1)}, f32[2,1,32,256]{3,2,1,0:T(8,128)S(1)}, bf16[2,224,256]{2,1,0:T(8,1...) custom-call(bf16[2,8,256,256]{3,2,1,0:T(8,128)(2,1)} %x2.3, ...), custom_call_target="tpu_custom_call" | custom-call | tf_op jit(solution)/shard_map/laterals/pallas_call | solution.py:299
  4.6 2.4 %collective-permute-start.2 = (bf16[2,256,256]{2,1,0:T(8,128)(2,1)S(1)}, bf16[2,256,256]{2,1,0:T(8,128)(2,1)S(1)}, u32[]{:S(2)}, u32[]{:S(2)}) collective-permute-start(bf16[2,256,256]{2,1,0:T(8,128)(2,1)S(1)} %get-tuple-element.28), channel_id=1, source_target_pairs={{0,1},{1,2},{2,3},{3,4},{4,5},{5,6},{6,7},{8,9},{9,10},{10,11},{11... | collective-permute-start | bytes 786440 | tf_op jit(solution)/shard_map/ppermute | solution.py:314
  7.0 1.3 %collective-permute-start.3 = (bf16[2,256,256]{2,1,0:T(8,128)(2,1)S(1)}, bf16[2,256,256]{2,1,0:T(8,128)(2,1)S(1)}, u32[]{:S(2)}, u32[]{:S(2)}) collective-permute-start(bf16[2,256,256]{2,1,0:T(8,128)(2,1)S(1)} %get-tuple-element.29), channel_id=1, source_target_pairs={{1,0},{2,1},{3,2},{4,3},{5,4},{6,5},{7,6},{9,8},{10,9},{11,10},{12... | collective-permute-start | bytes 786440 | tf_op jit(solution)/shard_map/ppermute | solution.py:315
  8.3 5.1 %collective-permute-start = (bf16[2,224,256]{2,1,0:T(8,128)(2,1)S(1)}, bf16[2,224,256]{2,1,0:T(8,128)(2,1)S(1)}, u32[]{:S(2)}, u32[]{:S(2)}) collective-permute-start(bf16[2,224,256]{2,1,0:T(8,128)(2,1)S(1)} %get-tuple-element.23), channel_id=1, source_target_pairs={{0,1},{1,2},{2,3},{3,4},{4,5},{5,6},{6,7},{8,9},{9,10},{10,11},{11... | collective-permute-start | bytes 688136 | tf_op jit(solution)/shard_map/ppermute | solution.py:314
  13.4 1.3 %collective-permute-start.1 = (bf16[2,224,256]{2,1,0:T(8,128)(2,1)S(1)}, bf16[2,224,256]{2,1,0:T(8,128)(2,1)S(1)}, u32[]{:S(2)}, u32[]{:S(2)}) collective-permute-start(bf16[2,224,256]{2,1,0:T(8,128)(2,1)S(1)} %get-tuple-element.24), channel_id=1, source_target_pairs={{1,0},{2,1},{3,2},{4,3},{5,4},{6,5},{7,6},{9,8},{10,9},{11,10},{12... | collective-permute-start | bytes 688136 | tf_op jit(solution)/shard_map/ppermute | solution.py:315
  14.7 0.1 add_convert_fusion.ends
  14.8 0.0 collective-permute-done.above
  14.8 3.2 %collective-permute-done.1.below = bf16[2,224,256]{2,1,0:T(8,128)(2,1)S(1)} collective-permute-done((bf16[2,224,256]{2,1,0:T(8,128)(2,1)S(1)}, bf16[2,224,256]{2,1,0:T(8,128)(2,1)S(1)}, u32[]{:S(2)}, u32[]{:S(2)}) %collective-permute-start.1) | collective-permute-done | bytes 229408 | tf_op jit(solution)/shard_map/ppermute | solution.py:315
  18.0 0.0 copy-done
  18.0 8.9 %merge_coarse.1 = (f32[2,4,128,256]{3,2,1,0:T(8,128)S(1)}, f32[2,2,64,256]{3,2,1,0:T(8,128)S(1)}, f32[2,1,32,256]{3,2,1,0:T(8,128)S(1)}, f32[12,256]{1,0:T(8,128...) custom-call(s32[2]{0:T(128)S(1)} %add_convert_fusion.ends, ...), custom_call_target="tpu_custom_call" | custom-call | tf_op jit(solution)/shard_map/merge_coarse/pallas_call | solution.py:321
  26.9 0.0 collective-permute-done.2.above2
  26.9 0.0 collective-permute-done.3.below2
  27.0 0.0 copy-start.1
  27.0 0.0 copy-start.2
  27.0 5.6 %conv_fine.1 = (f32[2,8,256,256]{3,2,1,0:T(8,128)S(1)}, f32[16,256]{1,0:T(8,128)S(1)}) custom-call(s32[2]{0:T(128)S(1)} %add_convert_fusion.ends, bf16[2,8,256,768]{3,2,1,0:T(8,128)(2,1)S(1)} %get-tuple-element.25.cat2, f32[2,2,256,256]{3,2,1,0:T(8,128)S(1)} %get-tuple-element.26.rim2, bf16[3,768,256]{2,1,0:T(8,128)(2,1)S(1)} %get-tuple-element.27.sw2, ...), custom_call_target="tpu_custom_call" | custom-call | tf_op jit(solution)/shard_map/conv_fine/pallas_call | solution.py:340
  32.6 5.1 %collective-permute-start.4 = (f32[16,256]{1,0:T(8,128)S(1)}, f32[16,256]{1,0:T(8,128)S(1)}, u32[]{:S(2)}, u32[]{:S(2)}) collective-permute-start(f32[16,256]{1,0:T(8,128)S(1)} %get-tuple-element.35), channel_id=1, source_target_pairs={{0,1},{1,0},{2,3},{3,2},{4,5},{5,4},{6,7},{7,6},{8,9},{9,8},{10,11... | collective-permute-start | bytes 49160 | tf_op jit(solution)/shard_map/ppermute | solution.py:269
  37.7 0.8 %collective-permute-done.4 = f32[16,256]{1,0:T(8,128)S(1)} collective-permute-done((f32[16,256]{1,0:T(8,128)S(1)}, f32[16,256]{1,0:T(8,128)S(1)}, u32[]{:S(2)}, u32[]{:S(2)}) %collective-permute-start.4) | collective-permute-done | bytes 16416 | tf_op jit(solution)/shard_map/ppermute | solution.py:269
  38.5 2.7 %collective-permute-start.5 = (f32[16,256]{1,0:T(8,128)S(1)}, f32[16,256]{1,0:T(8,128)S(1)}, u32[]{:S(2)}, u32[]{:S(2)}) collective-permute-start(f32[16,256]{1,0:T(8,128)S(1)} %add.9), channel_id=1, source_target_pairs={{0,2},{1,3},{2,0},{3,1},{4,6},{5,7},{6,4},{7,5},{8,10},{9,11},{10,... | collective-permute-start | bytes 49160 | tf_op jit(solution)/shard_map/ppermute | solution.py:269
  41.2 1.7 %collective-permute-done.5 = f32[16,256]{1,0:T(8,128)S(1)} collective-permute-done((f32[16,256]{1,0:T(8,128)S(1)}, f32[16,256]{1,0:T(8,128)S(1)}, u32[]{:S(2)}, u32[]{:S(2)}) %collective-permute-start.5) | collective-permute-done | bytes 16416 | tf_op jit(solution)/shard_map/ppermute | solution.py:269
  43.0 0.6 %collective-permute-start.6 = (f32[16,256]{1,0:T(8,128)S(1)}, f32[16,256]{1,0:T(8,128)S(1)}, u32[]{:S(2)}, u32[]{:S(2)}) collective-permute-start(f32[16,256]{1,0:T(8,128)S(1)} %add.10), channel_id=1, source_target_pairs={{0,4},{1,5},{2,6},{3,7},{4,0},{5,1},{6,2},{7,3},{8,12},{9,13},{10,... | collective-permute-start | bytes 49160 | tf_op jit(solution)/shard_map/ppermute | solution.py:269
  43.6 3.1 %collective-permute-done.6 = f32[16,256]{1,0:T(8,128)S(1)} collective-permute-done((f32[16,256]{1,0:T(8,128)S(1)}, f32[16,256]{1,0:T(8,128)S(1)}, u32[]{:S(2)}, u32[]{:S(2)}) %collective-permute-start.6) | collective-permute-done | bytes 16416 | tf_op jit(solution)/shard_map/ppermute | solution.py:269
  46.7 0.0 copy-done.1
  46.7 0.0 copy-done.2
  46.7 2.4 %normalize.1 = (bf16[2,8,256,256]{3,2,1,0:T(8,128)(2,1)}, bf16[2,4,128,256]{3,2,1,0:T(8,128)(2,1)}, bf16[2,2,64,256]{3,2,1,0:T(8,128)(2,1)}, bf16[2,1,32,256]{3,2,1,0:T(8,128)(2,1)}) custom-call(f32[2,8,256,256]{3,2,1,0:T(8,128)S(1)} %get-tuple-element.31.conv2, f32[2,4,128,256]{3,2,1,0:T(8,128)S(1)} %get-tuple-element.32.conv3, ...), custom_call_target="tpu_custom_call" | custom-call | tf_op jit(solution)/shard_map/normalize/pallas_call | solution.py:354
  (3 shorter events, 0.0 us)
Async XLA Ops:
  0.6 17.4 %copy-start = (f32[4,256]{1,0:T(4,128)S(1)}, f32[4,256]{1,0:T(4,128)}, u32[]{:S(2)}) copy-start(f32[4,256]{1,0:T(4,128)} %bias.3) | copy-start | bytes 12292
  4.6 22.4 %collective-permute-start.2 = (bf16[2,256,256]{2,1,0:T(8,128)(2,1)S(1)}, bf16[2,256,256]{2,1,0:T(8,128)(2,1)S(1)}, u32[]{:S(2)}, u32[]{:S(2)}) collective-permute-start(bf16[2,256,256]{2,1,0:T(8,128)(2,1)S(1)} %get-tuple-element.28), channel_id=1, source_target_pairs={{0,1},{1,2},{2,3},{3,4},{4,5},{5,6},{6,7},{8,9},{9,10},{10,11},{11... | collective-permute-start | bytes 786440 | tf_op jit(solution)/shard_map/ppermute | solution.py:314
  7.0 20.0 %collective-permute-start.3 = (bf16[2,256,256]{2,1,0:T(8,128)(2,1)S(1)}, bf16[2,256,256]{2,1,0:T(8,128)(2,1)S(1)}, u32[]{:S(2)}, u32[]{:S(2)}) collective-permute-start(bf16[2,256,256]{2,1,0:T(8,128)(2,1)S(1)} %get-tuple-element.29), channel_id=1, source_target_pairs={{1,0},{2,1},{3,2},{4,3},{5,4},{6,5},{7,6},{9,8},{10,9},{11,10},{12... | collective-permute-start | bytes 786440 | tf_op jit(solution)/shard_map/ppermute | solution.py:315
  8.3 6.5 %collective-permute-start = (bf16[2,224,256]{2,1,0:T(8,128)(2,1)S(1)}, bf16[2,224,256]{2,1,0:T(8,128)(2,1)S(1)}, u32[]{:S(2)}, u32[]{:S(2)}) collective-permute-start(bf16[2,224,256]{2,1,0:T(8,128)(2,1)S(1)} %get-tuple-element.23), channel_id=1, source_target_pairs={{0,1},{1,2},{2,3},{3,4},{4,5},{5,6},{6,7},{8,9},{9,10},{10,11},{11... | collective-permute-start | bytes 688136 | tf_op jit(solution)/shard_map/ppermute | solution.py:314
  13.4 4.6 %collective-permute-start.1 = (bf16[2,224,256]{2,1,0:T(8,128)(2,1)S(1)}, bf16[2,224,256]{2,1,0:T(8,128)(2,1)S(1)}, u32[]{:S(2)}, u32[]{:S(2)}) collective-permute-start(bf16[2,224,256]{2,1,0:T(8,128)(2,1)S(1)} %get-tuple-element.24), channel_id=1, source_target_pairs={{1,0},{2,1},{3,2},{4,3},{5,4},{6,5},{7,6},{9,8},{10,9},{11,10},{12... | collective-permute-start | bytes 688136 | tf_op jit(solution)/shard_map/ppermute | solution.py:315
  27.0 19.7 %copy-start.1 = (f32[4,256]{1,0:T(4,128)S(1)}, f32[4,256]{1,0:T(4,128)}, u32[]{:S(2)}) copy-start(f32[4,256]{1,0:T(4,128)} %gain.1) | copy-start | bytes 12292
  27.0 19.7 %copy-start.2 = (f32[4,256]{1,0:T(4,128)S(1)}, f32[4,256]{1,0:T(4,128)}, u32[]{:S(2)}) copy-start(f32[4,256]{1,0:T(4,128)} %shift.1) | copy-start | bytes 12292
  32.6 6.0 %collective-permute-start.4 = (f32[16,256]{1,0:T(8,128)S(1)}, f32[16,256]{1,0:T(8,128)S(1)}, u32[]{:S(2)}, u32[]{:S(2)}) collective-permute-start(f32[16,256]{1,0:T(8,128)S(1)} %get-tuple-element.35), channel_id=1, source_target_pairs={{0,1},{1,0},{2,3},{3,2},{4,5},{5,4},{6,7},{7,6},{8,9},{9,8},{10,11... | collective-permute-start | bytes 49160 | tf_op jit(solution)/shard_map/ppermute | solution.py:269
  38.5 4.4 %collective-permute-start.5 = (f32[16,256]{1,0:T(8,128)S(1)}, f32[16,256]{1,0:T(8,128)S(1)}, u32[]{:S(2)}, u32[]{:S(2)}) collective-permute-start(f32[16,256]{1,0:T(8,128)S(1)} %add.9), channel_id=1, source_target_pairs={{0,2},{1,3},{2,0},{3,1},{4,6},{5,7},{6,4},{7,5},{8,10},{9,11},{10,... | collective-permute-start | bytes 49160 | tf_op jit(solution)/shard_map/ppermute | solution.py:269
  43.0 3.7 %collective-permute-start.6 = (f32[16,256]{1,0:T(8,128)S(1)}, f32[16,256]{1,0:T(8,128)S(1)}, u32[]{:S(2)}, u32[]{:S(2)}) collective-permute-start(f32[16,256]{1,0:T(8,128)S(1)} %add.10), channel_id=1, source_target_pairs={{0,4},{1,5},{2,6},{3,7},{4,0},{5,1},{6,2},{7,3},{8,12},{9,13},{10,... | collective-permute-start | bytes 49160 | tf_op jit(solution)/shard_map/ppermute | solution.py:269
where the time goes:
time: 49.4 us; the launch traced here: 49.1 us
  Pallas kernels  20.8 us (42%)
  starting transfers between devices  18.6 us (38%)
  waiting for transfers between devices  8.88 us (18%)
  between operations  0.74 us (1%)
    pallas_call x1, Pallas kernels, per_device(): pl.pallas_call(coarse_kernel, out_shape=(maps[1], maps[2], maps[3], shape...  8.89 us
    ppermute x3, starting transfers between devices, total_over(): x = x + lax.ppermute(x, axis, [(i, i ^ step) for i in range(count)])  8.44 us
    ppermute x2, starting transfers between devices, per_device(): lax.ppermute(v, 'rows', [(i, i + 1) for i in range(ends)])  7.54 us
    ppermute x3, waiting for transfers between devices, total_over(): x = x + lax.ppermute(x, axis, [(i, i ^ step) for i in range(count)])  5.65 us
    pallas_call x1, Pallas kernels, per_device(): pl.pallas_call(fine_kernel, out_shape=(maps[0], shape((8 * images, channe...  5.61 us
    pallas_call x1, Pallas kernels, per_device(): pl.pallas_call(lateral_kernel, out_shape=(maps[1], maps[2], maps[3], pack...  3.92 us
    ppermute x2, waiting for transfers between devices, per_device(): lax.ppermute(v, 'rows', [(i + 1, i) for i in range(ends)])  3.23 us
    ppermute x2, starting transfers between devices, per_device(): lax.ppermute(v, 'rows', [(i + 1, i) for i in range(ends)])  2.58 us
  transfers between devices with their start and end apart: 7, of which 4 were waited for; matrix products, arithmetic and copies ran while one was open for 0% of the time, Pallas kernels for 18%

commit v1 on v0

--- a/solution.py
+++ b/solution.py
@@ -33,7 +33,7 @@
 
 def lateral_kernel(
     x2, x3, x4, x5, w2, w3, w4, w5, bias,
-    lat3, lat4, lat5, downward, upward, downward2, upward2,
+    lat3, lat4, lat5, downward, upward, downward2, upward2, u2, u3, u4,
     edge2, v3, v4, v5, m2, m3, m4, m5, offset, sems,
 ):
     rows2 = x2.shape[1]
@@ -49,6 +49,8 @@
         c.start()
     widths = (x3.shape[2], x4.shape[2], x5.shape[2])
     offsets, _ = segments(widths)
+    for table in (u4, u3, u2):
+        fill_weights(table)
     copies[9].wait()
     first = 0
     for level, v, m, out in ((3, v5, m5, lat5), (2, v4, m4, lat4), (1, v3, m3, lat3)):
@@ -101,9 +103,9 @@
 
 
 def coarse_kernel(
-    ends, x2, w2, bias, lat3, lat4, lat5, above, below, smooth,
+    ends, x2, w2, bias, lat3, lat4, lat5, u2, u3, u4, above, below, smooth,
     conv3, conv4, conv5, stats, cat2, rim2, sw2,
-    v2, m2, sw, cat3, cat4, cat5, u2, u3, u4, sems,
+    v2, m2, sw, cat3, cat4, cat5, sems,
 ):
     copies = [pltpu.make_async_copy(w2, m2, sems.at[0])]
     images, rows2, _, _ = x2.shape
@@ -125,8 +127,6 @@
     tables = (u2, u3, u4)
     lats = (None, lat3, lat4, lat5)
     channels = lat3.shape[-1]
-    for table in tables:
-        fill_weights(table)
     offsets, _ = segments(tuple(cat.shape[2] for cat in cats[1:]))
 
     def raised(level, image, start, which):
@@ -136,44 +136,46 @@
     for level in (3, 2, 1):
         height, cols = lats[level].shape[1:3]
         seg = slice(offsets[level - 1], offsets[level - 1] + cols)
-        for image in range(images):
-            for slot, source, gone, which in (
-                (0, above, is_first, 1),
-                (height + 1, below, is_last, 0),
-            ):
+        for slot, source, gone, which in (
+            (0, above, is_first, 1),
+            (height + 1, below, is_last, 0),
+        ):
+            for image in range(images):
                 acc = source[image, seg, :].astype(F32)
                 if level < 3:
                     acc = acc + raised(level, image, slot // 2, which)
                 put(cats[level], image, slot, jnp.where(gone, 0.0, acc))
-            for f in range(height):
+        for f in range(height):
+            which = f % 2
+            if f == 0:
+                which = jnp.where(is_first, 2, which)
+            if f == height - 1:
+                which = jnp.where(is_last, 3, which)
+            for image in range(images):
                 acc = lats[level][image, f]
                 if level < 3:
-                    which = f % 2
-                    if f == 0:
-                        which = jnp.where(is_first, 2, which)
-                    if f == height - 1:
-                        which = jnp.where(is_last, 3, which)
                     acc = acc + raised(level, image, (f + 1) // 2, which)
                 put(cats[level], image, f + 1, acc)
-    copies[0].wait()
     for image in range(images):
         rim2[0, image] = raised(0, image, 0, 1)
         rim2[1, image] = raised(0, image, rows2 // 2, 0)
-        copies[1 + image].wait()
-
-        def pair_rows(j, carry, image=image):
-            for odd in range(2):
-                f = 2 * j + odd
-                if odd:
-                    which = jnp.where(jnp.logical_and(is_last, f == rows2 - 1), 3, 1)
-                else:
-                    which = jnp.where(jnp.logical_and(is_first, f == 0), 2, 0)
+    for n in range(1 + images):
+        copies[n].wait()
+
+    def pair_rows(j, carry):
+        for odd in range(2):
+            f = 2 * j + odd
+            if odd:
+                which = jnp.where(jnp.logical_and(is_last, f == rows2 - 1), 3, 1)
+            else:
+                which = jnp.where(jnp.logical_and(is_first, f == 0), 2, 0)
+            for image in range(images):
                 acc = dot(v2[image, f], m2[...]) + bias[0:1, :]
                 acc = acc + raised(0, image, j + odd, which)
                 put(cat2, image, f, acc)
-            return carry
-
-        lax.fori_loop(0, rows2 // 2, pair_rows, 0)
+        return carry
+
+    lax.fori_loop(0, rows2 // 2, pair_rows, 0)
 
     for level, out in ((1, conv3), (2, conv4), (3, conv5)):
         copies[images + level].wait()
@@ -296,11 +298,13 @@
     maps = [shape((images, heights[k], widths[k], channels), F32) for k in range(4)]
     packed = shape((images, pack, channels), BF16)
     packed2 = shape((images, widths[0], channels), BF16)
-    lat3, lat4, lat5, downward, upward, downward2, upward2 = pl.pallas_call(
+    table = lambda k: shape((4, widths[k], 2 * widths[k + 1]), BF16)
+    lat3, lat4, lat5, downward, upward, downward2, upward2, *tables = pl.pallas_call(
         lateral_kernel,
-        out_shape=(maps[1], maps[2], maps[3], packed, packed, packed2, packed2),
+        out_shape=(maps[1], maps[2], maps[3], packed, packed, packed2, packed2)
+        + (table(0), table(1), table(2)),
         in_specs=[hbm] * 9,
-        out_specs=[vmem] * 7,
+        out_specs=[vmem] * 10,
         scratch_shapes=[
             pltpu.VMEM((2, images) + level_two.shape[2:], level_two.dtype),
             like(level_three), like(level_four), like(level_five),
@@ -317,7 +321,6 @@
     above2, below2 = from_above(downward2), from_below(upward2)
     flags = jnp.stack([position == 0, position == ends]).astype(jnp.int32)
     cat = lambda k: pltpu.VMEM((images, heights[k] + 2, widths[k], 3 * channels), BF16)
-    table = lambda k: pltpu.VMEM((4, widths[k], 2 * widths[k + 1]), BF16)
     conv3, conv4, conv5, coarse_stats, cat2, rim2, sw2 = pl.pallas_call(
         coarse_kernel,
         out_shape=(
@@ -326,17 +329,17 @@
             shape((2, images, widths[0], channels), F32),
             shape(smooth_weight.shape[1:], BF16),
         ),
-        in_specs=[smem, hbm, hbm] + [vmem] * 6 + [hbm],
+        in_specs=[smem, hbm, hbm] + [vmem] * 9 + [hbm],
         out_specs=[vmem] * 7,
         scratch_shapes=[
             like(level_two), like(lateral_two),
             pltpu.VMEM((3,) + smooth_weight.shape[1:], BF16),
-            cat(1), cat(2), cat(3), table(0), table(1), table(2),
+            cat(1), cat(2), cat(3),
             pltpu.SemaphoreType.DMA((5 + images,)),
         ],
         compiler_params=pltpu.CompilerParams(vmem_limit_bytes=24 * MIB),
         name="merge_coarse",
-    )(flags, levels[0], laterals[0], lateral_bias, lat3, lat4, lat5, above, below, smooth)
+    )(flags, levels[0], laterals[0], lateral_bias, lat3, lat4, lat5, *tables, above, below, smooth)
     conv2, stats = pl.pallas_call(
         fine_kernel,
         out_shape=(maps[0], shape((8 * images, channels), F32)),

time: 49.4 us -> 49.2 us (level)
    pallas_call x1, Pallas kernels: 8.89 us -> 7.78 us  [per_device(): pl.pallas_call(coarse_kernel, out_shape=(maps[1], maps[2], maps[3], shape...]
    pallas_call x1, Pallas kernels: 3.92 us -> 4.63 us  [per_device(): pl.pallas_call(lateral_kernel, out_shape=(maps[1], maps[2], maps[3], pack...]
  transfers between devices with their start and end apart: 7 -> 7, of which waited for: 4 -> 4; matrix products, arithmetic and copies ran while one was open for 0% -> 0% of each run, Pallas kernels for 18% -> 16%
where the time goes in v1:
time: 49.2 us; the launch traced here: 48.9 us
  Pallas kernels  20.4 us (41%)
  starting transfers between devices  18.7 us (38%)
  waiting for transfers between devices  8.99 us (18%)
  between operations  0.74 us (2%)
    ppermute x3, starting transfers between devices, total_over(): x = x + lax.ppermute(x, axis, [(i, i ^ step) for i in range(count)])  8.55 us
    pallas_call x1, Pallas kernels, per_device(): pl.pallas_call(coarse_kernel, out_shape=(maps[1], maps[2], maps[3], shape...  7.78 us
    ppermute x2, starting transfers between devices, per_device(): lax.ppermute(v, 'rows', [(i, i + 1) for i in range(ends)])  7.53 us
    pallas_call x1, Pallas kernels, per_device(): pl.pallas_call(fine_kernel, out_shape=(maps[0], shape((8 * images, channe...  5.6 us
    ppermute x3, waiting for transfers between devices, total_over(): x = x + lax.ppermute(x, axis, [(i, i ^ step) for i in range(count)])  5.55 us
    pallas_call x1, Pallas kernels, per_device(): pl.pallas_call(lateral_kernel, out_shape=(maps[1], maps[2], maps[3], pack...  4.63 us
    ppermute x2, waiting for transfers between devices, per_device(): lax.ppermute(v, 'rows', [(i + 1, i) for i in range(ends)])  3.44 us
    ppermute x2, starting transfers between devices, per_device(): lax.ppermute(v, 'rows', [(i + 1, i) for i in range(ends)])  2.58 us
  transfers between devices with their start and end apart: 7, of which 4 were waited for; matrix products, arithmetic and copies ran while one was open for 0% of the time, Pallas kernels for 16%

profile of v1, /device:TPU:0, one launch (start us, length us, event | category | flops | bytes accessed | tf_op | source)
XLA Modules:
  0.0 48.9 jit_solution(5033662379653700789)
XLA Ops:
  0.6 0.0 copy-start
  0.6 4.6 %laterals.1 = (f32[2,4,128,256]{3,2,1,0:T(8,128)S(1)}, f32[2,2,64,256]{3,2,1,0:T(8,128)S(1)}, f32[2,1,32,256]{3,2,1,0:T(8,128)S(1)}, bf16[2,224,256]{2,1,0:T(8,1...) custom-call(bf16[2,8,256,256]{3,2,1,0:T(8,128)(2,1)} %x2.3, ...), custom_call_target="tpu_custom_call" | custom-call | tf_op jit(solution)/shard_map/laterals/pallas_call | solution.py:302
  5.3 2.4 %collective-permute-start.2 = (bf16[2,256,256]{2,1,0:T(8,128)(2,1)}, bf16[2,256,256]{2,1,0:T(8,128)(2,1)S(1)}, u32[]{:S(2)}, u32[]{:S(2)}) collective-permute-start(bf16[2,256,256]{2,1,0:T(8,128)(2,1)} %get-tuple-element.34), channel_id=1, source_target_pairs={{0,1},{1,2},{2,3},{3,4},{4,5},{5,6},{6,7},{8,9},{9,10},{10,11},{11... | collective-permute-start | bytes 786440 | tf_op jit(solution)/shard_map/ppermute | solution.py:318
  7.7 1.3 %collective-permute-start.3 = (bf16[2,256,256]{2,1,0:T(8,128)(2,1)S(1)}, bf16[2,256,256]{2,1,0:T(8,128)(2,1)S(1)}, u32[]{:S(2)}, u32[]{:S(2)}) collective-permute-start(bf16[2,256,256]{2,1,0:T(8,128)(2,1)S(1)} %get-tuple-element.35), channel_id=1, source_target_pairs={{1,0},{2,1},{3,2},{4,3},{5,4},{6,5},{7,6},{9,8},{10,9},{11,10},{12... | collective-permute-start | bytes 786440 | tf_op jit(solution)/shard_map/ppermute | solution.py:319
  9.0 5.1 %collective-permute-start = (bf16[2,224,256]{2,1,0:T(8,128)(2,1)}, bf16[2,224,256]{2,1,0:T(8,128)(2,1)S(1)}, u32[]{:S(2)}, u32[]{:S(2)}) collective-permute-start(bf16[2,224,256]{2,1,0:T(8,128)(2,1)} %get-tuple-element.29), channel_id=1, source_target_pairs={{0,1},{1,2},{2,3},{3,4},{4,5},{5,6},{6,7},{8,9},{9,10},{10,11},{11... | collective-permute-start | bytes 688136 | tf_op jit(solution)/shard_map/ppermute | solution.py:318
  14.1 1.3 %collective-permute-start.1 = (bf16[2,224,256]{2,1,0:T(8,128)(2,1)}, bf16[2,224,256]{2,1,0:T(8,128)(2,1)S(1)}, u32[]{:S(2)}, u32[]{:S(2)}) collective-permute-start(bf16[2,224,256]{2,1,0:T(8,128)(2,1)} %get-tuple-element.30), channel_id=1, source_target_pairs={{1,0},{2,1},{3,2},{4,3},{5,4},{6,5},{7,6},{9,8},{10,9},{11,10},{12... | collective-permute-start | bytes 688136 | tf_op jit(solution)/shard_map/ppermute | solution.py:319
  15.4 0.1 add_convert_fusion.ends
  15.5 0.0 collective-permute-done.above
  15.5 3.4 %collective-permute-done.1.below = bf16[2,224,256]{2,1,0:T(8,128)(2,1)S(1)} collective-permute-done((bf16[2,224,256]{2,1,0:T(8,128)(2,1)}, bf16[2,224,256]{2,1,0:T(8,128)(2,1)S(1)}, u32[]{:S(2)}, u32[]{:S(2)}) %collective-permute-start.1) | collective-permute-done | bytes 229408 | tf_op jit(solution)/shard_map/ppermute | solution.py:319
  18.9 0.0 copy-done
  19.0 7.8 %merge_coarse.1 = (f32[2,4,128,256]{3,2,1,0:T(8,128)S(1)}, f32[2,2,64,256]{3,2,1,0:T(8,128)S(1)}, f32[2,1,32,256]{3,2,1,0:T(8,128)S(1)}, f32[12,256]{1,0:T(8,128...) custom-call(s32[2]{0:T(128)S(1)} %add_convert_fusion.ends, ...), custom_call_target="tpu_custom_call" | custom-call | tf_op jit(solution)/shard_map/merge_coarse/pallas_call | solution.py:324
  26.7 0.0 collective-permute-done.2.above2
  26.8 0.0 collective-permute-done.3.below2
  26.8 0.0 copy-start.1
  26.8 0.0 copy-start.2
  26.8 5.6 %conv_fine.1 = (f32[2,8,256,256]{3,2,1,0:T(8,128)S(1)}, f32[16,256]{1,0:T(8,128)S(1)}) custom-call(s32[2]{0:T(128)S(1)} %add_convert_fusion.ends, bf16[2,8,256,768]{3,2,1,0:T(8,128)(2,1)S(1)} %get-tuple-element.31.cat2, f32[2,2,256,256]{3,2,1,0:T(8,128)S(1)} %get-tuple-element.32.rim2, bf16[3,768,256]{2,1,0:T(8,128)(2,1)S(1)} %get-tuple-element.33.sw2, ...), custom_call_target="tpu_custom_call" | custom-call | tf_op jit(solution)/shard_map/conv_fine/pallas_call | solution.py:343
  32.4 5.1 %collective-permute-start.4 = (f32[16,256]{1,0:T(8,128)S(1)}, f32[16,256]{1,0:T(8,128)S(1)}, u32[]{:S(2)}, u32[]{:S(2)}) collective-permute-start(f32[16,256]{1,0:T(8,128)S(1)} %get-tuple-element.41), channel_id=1, source_target_pairs={{0,1},{1,0},{2,3},{3,2},{4,5},{5,4},{6,7},{7,6},{8,9},{9,8},{10,11... | collective-permute-start | bytes 49160 | tf_op jit(solution)/shard_map/ppermute | solution.py:271
  37.5 0.8 %collective-permute-done.4 = f32[16,256]{1,0:T(8,128)S(1)} collective-permute-done((f32[16,256]{1,0:T(8,128)S(1)}, f32[16,256]{1,0:T(8,128)S(1)}, u32[]{:S(2)}, u32[]{:S(2)}) %collective-permute-start.4) | collective-permute-done | bytes 16416 | tf_op jit(solution)/shard_map/ppermute | solution.py:271
  38.4 2.7 %collective-permute-start.5 = (f32[16,256]{1,0:T(8,128)S(1)}, f32[16,256]{1,0:T(8,128)S(1)}, u32[]{:S(2)}, u32[]{:S(2)}) collective-permute-start(f32[16,256]{1,0:T(8,128)S(1)} %add.9), channel_id=1, source_target_pairs={{0,2},{1,3},{2,0},{3,1},{4,6},{5,7},{6,4},{7,5},{8,10},{9,11},{10,... | collective-permute-start | bytes 49160 | tf_op jit(solution)/shard_map/ppermute | solution.py:271
  41.0 1.7 %collective-permute-done.5 = f32[16,256]{1,0:T(8,128)S(1)} collective-permute-done((f32[16,256]{1,0:T(8,128)S(1)}, f32[16,256]{1,0:T(8,128)S(1)}, u32[]{:S(2)}, u32[]{:S(2)}) %collective-permute-start.5) | collective-permute-done | bytes 16416 | tf_op jit(solution)/shard_map/ppermute | solution.py:271
  42.8 0.7 %collective-permute-start.6 = (f32[16,256]{1,0:T(8,128)S(1)}, f32[16,256]{1,0:T(8,128)S(1)}, u32[]{:S(2)}, u32[]{:S(2)}) collective-permute-start(f32[16,256]{1,0:T(8,128)S(1)} %add.10), channel_id=1, source_target_pairs={{0,4},{1,5},{2,6},{3,7},{4,0},{5,1},{6,2},{7,3},{8,12},{9,13},{10,... | collective-permute-start | bytes 49160 | tf_op jit(solution)/shard_map/ppermute | solution.py:271
  43.5 3.0 %collective-permute-done.6 = f32[16,256]{1,0:T(8,128)S(1)} collective-permute-done((f32[16,256]{1,0:T(8,128)S(1)}, f32[16,256]{1,0:T(8,128)S(1)}, u32[]{:S(2)}, u32[]{:S(2)}) %collective-permute-start.6) | collective-permute-done | bytes 16416 | tf_op jit(solution)/shard_map/ppermute | solution.py:271
  46.5 0.0 copy-done.1
  46.5 0.0 copy-done.2
  46.5 2.4 %normalize.1 = (bf16[2,8,256,256]{3,2,1,0:T(8,128)(2,1)}, bf16[2,4,128,256]{3,2,1,0:T(8,128)(2,1)}, bf16[2,2,64,256]{3,2,1,0:T(8,128)(2,1)}, bf16[2,1,32,256]{3,2,1,0:T(8,128)(2,1)}) custom-call(f32[2,8,256,256]{3,2,1,0:T(8,128)S(1)} %get-tuple-element.37.conv2, f32[2,4,128,256]{3,2,1,0:T(8,128)S(1)} %get-tuple-element.38.conv3, ...), custom_call_target="tpu_custom_call" | custom-call | tf_op jit(solution)/shard_map/normalize/pallas_call | solution.py:357
  (3 shorter events, 0.0 us)
Async XLA Ops:
  0.6 18.3 %copy-start = (f32[4,256]{1,0:T(4,128)S(1)}, f32[4,256]{1,0:T(4,128)}, u32[]{:S(2)}) copy-start(f32[4,256]{1,0:T(4,128)} %bias.3) | copy-start | bytes 12292
  5.3 21.5 %collective-permute-start.2 = (bf16[2,256,256]{2,1,0:T(8,128)(2,1)}, bf16[2,256,256]{2,1,0:T(8,128)(2,1)S(1)}, u32[]{:S(2)}, u32[]{:S(2)}) collective-permute-start(bf16[2,256,256]{2,1,0:T(8,128)(2,1)} %get-tuple-element.34), channel_id=1, source_target_pairs={{0,1},{1,2},{2,3},{3,4},{4,5},{5,6},{6,7},{8,9},{9,10},{10,11},{11... | collective-permute-start | bytes 786440 | tf_op jit(solution)/shard_map/ppermute | solution.py:318
  7.7 19.1 %collective-permute-start.3 = (bf16[2,256,256]{2,1,0:T(8,128)(2,1)S(1)}, bf16[2,256,256]{2,1,0:T(8,128)(2,1)S(1)}, u32[]{:S(2)}, u32[]{:S(2)}) collective-permute-start(bf16[2,256,256]{2,1,0:T(8,128)(2,1)S(1)} %get-tuple-element.35), channel_id=1, source_target_pairs={{1,0},{2,1},{3,2},{4,3},{5,4},{6,5},{7,6},{9,8},{10,9},{11,10},{12... | collective-permute-start | bytes 786440 | tf_op jit(solution)/shard_map/ppermute | solution.py:319
  9.0 6.5 %collective-permute-start = (bf16[2,224,256]{2,1,0:T(8,128)(2,1)}, bf16[2,224,256]{2,1,0:T(8,128)(2,1)S(1)}, u32[]{:S(2)}, u32[]{:S(2)}) collective-permute-start(bf16[2,224,256]{2,1,0:T(8,128)(2,1)} %get-tuple-element.29), channel_id=1, source_target_pairs={{0,1},{1,2},{2,3},{3,4},{4,5},{5,6},{6,7},{8,9},{9,10},{10,11},{11... | collective-permute-start | bytes 688136 | tf_op jit(solution)/shard_map/ppermute | solution.py:318
  14.1 4.8 %collective-permute-start.1 = (bf16[2,224,256]{2,1,0:T(8,128)(2,1)}, bf16[2,224,256]{2,1,0:T(8,128)(2,1)S(1)}, u32[]{:S(2)}, u32[]{:S(2)}) collective-permute-start(bf16[2,224,256]{2,1,0:T(8,128)(2,1)} %get-tuple-element.30), channel_id=1, source_target_pairs={{1,0},{2,1},{3,2},{4,3},{5,4},{6,5},{7,6},{9,8},{10,9},{11,10},{12... | collective-permute-start | bytes 688136 | tf_op jit(solution)/shard_map/ppermute | solution.py:319
  26.8 19.8 %copy-start.1 = (f32[4,256]{1,0:T(4,128)S(1)}, f32[4,256]{1,0:T(4,128)}, u32[]{:S(2)}) copy-start(f32[4,256]{1,0:T(4,128)} %gain.1) | copy-start | bytes 12292
  26.8 19.7 %copy-start.2 = (f32[4,256]{1,0:T(4,128)S(1)}, f32[4,256]{1,0:T(4,128)}, u32[]{:S(2)}) copy-start(f32[4,256]{1,0:T(4,128)} %shift.1) | copy-start | bytes 12292
  32.4 6.0 %collective-permute-start.4 = (f32[16,256]{1,0:T(8,128)S(1)}, f32[16,256]{1,0:T(8,128)S(1)}, u32[]{:S(2)}, u32[]{:S(2)}) collective-permute-start(f32[16,256]{1,0:T(8,128)S(1)} %get-tuple-element.41), channel_id=1, source_target_pairs={{0,1},{1,0},{2,3},{3,2},{4,5},{5,4},{6,7},{7,6},{8,9},{9,8},{10,11... | collective-permute-start | bytes 49160 | tf_op jit(solution)/shard_map/ppermute | solution.py:271
  38.4 4.4 %collective-permute-start.5 = (f32[16,256]{1,0:T(8,128)S(1)}, f32[16,256]{1,0:T(8,128)S(1)}, u32[]{:S(2)}, u32[]{:S(2)}) collective-permute-start(f32[16,256]{1,0:T(8,128)S(1)} %add.9), channel_id=1, source_target_pairs={{0,2},{1,3},{2,0},{3,1},{4,6},{5,7},{6,4},{7,5},{8,10},{9,11},{10,... | collective-permute-start | bytes 49160 | tf_op jit(solution)/shard_map/ppermute | solution.py:271
  42.8 3.7 %collective-permute-start.6 = (f32[16,256]{1,0:T(8,128)S(1)}, f32[16,256]{1,0:T(8,128)S(1)}, u32[]{:S(2)}, u32[]{:S(2)}) collective-permute-start(f32[16,256]{1,0:T(8,128)S(1)} %add.10), channel_id=1, source_target_pairs={{0,4},{1,5},{2,6},{3,7},{4,0},{5,1},{6,2},{7,3},{8,12},{9,13},{10,... | collective-permute-start | bytes 49160 | tf_op jit(solution)/shard_map/ppermute | solution.py:271
